TPU v7x, 32 devices: a whole 2x2x4 slice. The times are simulated.
32 devices in a mesh: groups: 2 (over x), seq: 16 (over z, y, core).
Axes of the slice: x: 2, y: 2, z: 4, core: 2. Of those that a mesh axis runs over, the one named last changes fastest.
Arguments:
- queries: bfloat16 [8192, 4096], P(('groups', 'seq')), parts along dimension 0, may hold values from -6 to 6
- keys: bfloat16 [8192, 2048], P(('groups', 'seq')), parts along dimension 0, may hold values from -6 to 6
- values: bfloat16 [8192, 2048], P(('groups', 'seq')), parts along dimension 0, may hold values from -6 to 6
- doc_blocks: int32 [16], P('groups'), parts along dimension 0, may hold values from 1 to 8, 32 in all
Outputs:
- attended: bfloat16 [8192, 4096], P(('groups', 'seq')), parts along dimension 0
There are 2 independent parts, one for each index of `groups`. A program takes and returns all parts, laid end to end along the dimension named above; each array names one. Nothing has to cross between parts.
Inputs may be any that keep to these rules, and one draw needn't show every extreme that they name: `doc_blocks`: the lengths add up to 32; the longest document has exactly 8 units.
All inputs are finite; a program needn't handle non-finite values.
Results may differ from a plain program's by a relative error of at most 0.004.
Values may be sent and summed in bfloat16 or wider, within the bound.
A program may use at most 64 MiB of HBM per device.

v0:
```python
import functools

import jax
import jax.numpy as jnp
from jax import lax
from jax.experimental import pallas as pl
from jax.experimental.pallas import tpu as pltpu
from jax.sharding import PartitionSpec as P

DH = 128
BLK = 128
CHUNK_HEADS = 1
ROUTED = 1
EXP2_SCALE = 144.0 ** (-0.5) * 1.4426950408889634
HIDDEN = -1e30
ROUTED_STEP = 6
CROSS_AHEAD = 4
UP_AHEAD = 3


def kernel(
    n,
    window,
    docs_ref,
    q_hbm,
    k_hbm,
    v_hbm,
    o_own,
    q_own,
    k_own,
    v_own,
    k_halo,
    v_halo,
    local_sem,
    send_sem,
    recv_sem,
    k_transit,
    v_transit,
    transit_send,
    transit_recv,
    forward_send,
):
    me = lax.axis_index("seq")
    pairs = window // 2
    place = lax.rem(me, window)
    base = me - place
    pair = place // 2
    core = lax.rem(me, 2)
    partner = me + 1 - 2 * core
    above = me + window
    below = me - window
    has_above = above < n
    has_below = below >= 0

    rows, kv_width = k_hbm.shape
    ratio = q_hbm.shape[1] // kv_width
    width = CHUNK_HEADS * DH
    chunks = kv_width // width
    blocks = rows // BLK
    own_hbm = (k_hbm, v_hbm)
    halo = (k_halo, v_halo)
    transit = (k_transit, v_transit)
    first_routed = chunks - ROUTED

    def pair_device(step):
        return base + 2 * lax.rem(pair + step, pairs) + core

    def kv_cols(c):
        return pl.ds(pl.multiple_of(c * width, width), width)

    def remote_one(kind, c, src_slot, dst_slot, device, from_row=0):
        taken = pl.ds(from_row, rows - from_row)
        if src_slot is None:
            src = own_hbm[kind].at[taken, kv_cols(c)]
        else:
            src = halo[kind].at[src_slot, taken, kv_cols(c)]
        return pltpu.make_async_remote_copy(
            src_ref=src,
            dst_ref=halo[kind].at[dst_slot, taken, kv_cols(c)],
            send_sem=send_sem.at[kind, dst_slot, c],
            recv_sem=recv_sem.at[kind, dst_slot, c],
            device_id={"seq": device},
            device_id_type=pl.DeviceIdType.MESH,
        )

    def is_routed(c):
        return (c >= first_routed) & (c < first_routed + ROUTED)

    def turn(spot):
        moved = jnp.where(spot < chunks - 1, spot + 1, first_routed - 1)
        return jnp.where((pair == 0) & (spot >= first_routed - 1), moved, spot)

    def across(kind, c, step):
        spot = c - first_routed
        return pltpu.make_async_remote_copy(
            src_ref=own_hbm[kind].at[:, kv_cols(c)],
            dst_ref=transit[kind].at[step - 1, spot],
            send_sem=transit_send.at[kind, step - 1, spot],
            recv_sem=transit_recv.at[kind, step - 1, spot],
            device_id={"seq": pair_device(step)},
            device_id_type=pl.DeviceIdType.MESH,
        )

    def forward(kind, c, step):
        spot = c - first_routed
        return pltpu.make_async_remote_copy(
            src_ref=transit[kind].at[step - 1, spot],
            dst_ref=halo[kind].at[2 * step, :, kv_cols(c)],
            send_sem=forward_send.at[kind, step - 1, spot],
            recv_sem=recv_sem.at[kind, 2 * step, c],
            device_id={"seq": above},
            device_id_type=pl.DeviceIdType.MESH,
        )

    def remote(c, src_slot, dst_slot, device):
        return [remote_one(kind, c, src_slot, dst_slot, device) for kind in range(2)]

    def upward(kind, c, act):
        @pl.when(place == 0)
        def _():
            act(remote_one(kind, c, None, 0, above, BLK))

        @pl.when(place != 0)
        def _():
            act(remote_one(kind, c, None, 0, above))

    def start(copies):
        for copy in copies:
            copy.start()

    def partner_slot(step):
        return lax.rem(2 * step + 1 - 2 * core + window, window)

    barrier = pltpu.get_barrier_semaphore()

    def greet(device):
        pl.semaphore_signal(
            barrier, inc=1, device_id={"seq": device}, device_id_type=pl.DeviceIdType.MESH
        )

    greet(partner)
    for step in range(1, pairs):
        greet(pair_device(step))

    @pl.when(has_above)
    def _():
        greet(above)

    @pl.when(has_below)
    def _():
        greet(below)

    local = [
        pltpu.make_async_copy(k_hbm, k_own, local_sem.at[0]),
        pltpu.make_async_copy(v_hbm, v_own, local_sem.at[1]),
        pltpu.make_async_copy(q_hbm, q_own, local_sem.at[2]),
    ]
    start(local)
    pl.semaphore_wait(
        barrier, pairs + has_above.astype(jnp.int32) + has_below.astype(jnp.int32)
    )

    def cross_first(spot, carry):
        for step in range(1, pairs):

            @pl.when((pair + step >= pairs) & has_above)
            def _():
                for kind in range(2):
                    across(kind, first_routed + spot, step).start()

        return carry

    lax.fori_loop(0, ROUTED, cross_first, 0)

    def first_sends(c, carry):
        @pl.when(has_above)
        def _():
            for kind in range(2):
                upward(kind, c, lambda copy: copy.start())

        for step in range(1, pairs):

            @pl.when(pair + step < pairs)
            def _():
                start(remote(c, None, 2 * step, pair_device(step)))

        @pl.when(core == 0)
        def _():
            start(remote(c, None, 1, partner))

        return carry

    lax.fori_loop(0, chunks, first_sends, 0)

    @pl.when(jnp.logical_not(has_below))
    def _():
        for r in range(window):

            @pl.when((r == 0) | (r > place))
            def _():
                def clear(i, carry):
                    taken = pl.ds(pl.multiple_of(i * 16, 16), 16)
                    for ref in halo:
                        ref[r, taken, :] = jnp.zeros((16, kv_width), ref.dtype)
                    return carry

                lax.fori_loop(0, rows // 16, clear, 0)

    hide_rows = []
    for a in range(blocks):
        number = me * blocks + a
        end = jnp.int32(0)
        first = jnp.int32(0)
        for d in range(docs_ref.shape[0]):
            end = end + docs_ref[d]
            first = jnp.where(end <= number, end, first)
        held = [(me - window) * blocks + b for b in range(a + 1, blocks)]
        for r in range(1, window):
            held += [(me - r) * blocks + b for b in range(blocks)]
        held += [me * blocks + b for b in range(a + 1)]
        hide_rows.append(
            jnp.concatenate(
                [
                    jnp.full((1, BLK), jnp.where(b >= first, 0.0, HIDDEN), jnp.float32)
                    for b in held
                ],
                axis=1,
            )
        )

    for copy in local:
        copy.wait()

    def attend(c):
        q_index = lax.broadcasted_iota(jnp.int32, (BLK, BLK), 0)
        k_index = lax.broadcasted_iota(jnp.int32, (BLK, BLK), 1)
        causal = jnp.where(k_index <= q_index, 0.0, HIDDEN).astype(jnp.float32)
        causal = jnp.concatenate([causal] * ratio, axis=0)
        for h in range(CHUNK_HEADS):
            cols = pl.ds(pl.multiple_of(c * width + h * DH, DH), DH)
            for a in range(blocks):
                own_rows = (a + 1) * BLK

                def gathered(halo_ref, own_ref):
                    parts = []
                    if own_rows < rows:
                        parts.append(halo_ref[0, own_rows:, cols])
                    for r in range(1, window):
                        parts.append(halo_ref[r, :, cols])
                    parts.append(own_ref[:own_rows, cols])
                    return jnp.concatenate(parts, axis=0)

                head_cols = [
                    pl.ds(pl.multiple_of((c * width + h * DH) * ratio + g * DH, DH), DH)
                    for g in range(ratio)
                ]
                tile_rows = slice(a * BLK, (a + 1) * BLK)
                q_tile = jnp.concatenate([q_own[tile_rows, hc] for hc in head_cols], axis=0)
                scores = lax.dot_general(
                    q_tile,
                    gathered(k_halo, k_own),
                    (((1,), (1,)), ((), ())),
                    preferred_element_type=jnp.float32,
                )
                scores = scores + hide_rows[a]
                scores = jnp.concatenate([scores[:, :-BLK], scores[:, -BLK:] + causal], axis=1)
                top = jnp.max(scores, axis=1, keepdims=True)
                weights = jnp.exp2((scores - top) * EXP2_SCALE)
                total = jnp.sum(weights, axis=1, keepdims=True)
                blended = jnp.dot(
                    weights.astype(jnp.bfloat16),
                    gathered(v_halo, v_own),
                    preferred_element_type=jnp.float32,
                )
                blended = (blended / total).astype(o_own.dtype)
                for g in range(ratio):
                    o_own[tile_rows, head_cols[g]] = blended[g * BLK : (g + 1) * BLK]

    def arrived(c, slot):
        for copy in remote(c, None, slot, partner):
            copy.wait_recv()

    def step_of(t, carry):
        @pl.when((t < chunks) & has_below)
        def _():
            c = t
            for kind in range(2):
                upward(kind, c, lambda copy: copy.wait_recv())

                @pl.when(core == 1)
                def _():
                    remote_one(kind, c, 0, window - 1, partner).start()

                for step in range(1, pairs):

                    @pl.when((pair + step >= pairs) & jnp.logical_not(is_routed(c)))
                    def _():
                        remote_one(kind, c, 0, 2 * step, pair_device(step)).start()

        @pl.when((t < ROUTED) & has_above)
        def _():
            for step in range(1, pairs):

                @pl.when(step > pair)
                def _():
                    for kind in range(2):
                        across(kind, t + first_routed, step).wait_recv()
                        forward(kind, t + first_routed, step).start()

        @pl.when((t >= 1) & (t < chunks + 1))
        def _():
            c = turn(t - 1)
            for step in range(1, pairs):

                @pl.when((pair >= step) | has_below)
                def _():
                    for kind in range(2):
                        remote_one(kind, c, None, 2 * step, partner).wait_recv()
                        remote_one(kind, c, 2 * step, partner_slot(step), partner).start()

        @pl.when((t >= 2) & (t < chunks + 2))
        def _():
            c = turn(t - 2)
            for r in range(1, window, 2):

                @pl.when((place >= r) | has_below)
                def _():
                    arrived(c, r)

            attend(c)

        return carry

    lax.fori_loop(0, chunks + 2, step_of, 0)

    def finish(c, carry):
        def sent(slot):
            for copy in remote(c, None, slot, partner):
                copy.wait_send()

        @pl.when(has_above)
        def _():
            for kind in range(2):
                upward(kind, c, lambda copy: copy.wait_send())

        @pl.when((core == 0) | has_below)
        def _():
            sent(partner_slot(0))

        for step in range(1, pairs):

            @pl.when((pair + step < pairs) | (has_below & jnp.logical_not(is_routed(c))))
            def _():
                sent(2 * step)

            @pl.when((pair + step >= pairs) & has_above & is_routed(c))
            def _():
                for kind in range(2):
                    across(kind, c, step).wait_send()

            @pl.when((step > pair) & has_above & is_routed(c))
            def _():
                for kind in range(2):
                    forward(kind, c, step).wait_send()

            @pl.when((pair >= step) | has_below)
            def _():
                sent(partner_slot(step))

        return carry

    lax.fori_loop(0, chunks, finish, 0)


def on_device(n, queries, keys, values, doc_blocks):
    window = n // 4
    rows, kv_width = keys.shape
    chunks = kv_width // (CHUNK_HEADS * DH)
    return pl.pallas_call(
        functools.partial(kernel, n, window),
        out_shape=pltpu.VMEM(queries.shape, queries.dtype),
        in_specs=[pl.BlockSpec(memory_space=pltpu.SMEM)]
        + [pl.BlockSpec(memory_space=pl.ANY)] * 3,
        out_specs=pl.BlockSpec(memory_space=pltpu.VMEM),
        scratch_shapes=[
            pltpu.VMEM(queries.shape, queries.dtype),
            pltpu.VMEM(keys.shape, keys.dtype),
            pltpu.VMEM(values.shape, values.dtype),
            pltpu.VMEM((window, rows, kv_width), keys.dtype),
            pltpu.VMEM((window, rows, kv_width), values.dtype),
            pltpu.SemaphoreType.DMA((3,)),
            pltpu.SemaphoreType.DMA((2, window, chunks)),
            pltpu.SemaphoreType.DMA((2, window, chunks)),
            pltpu.VMEM((window // 2 - 1, ROUTED, rows, CHUNK_HEADS * DH), keys.dtype),
            pltpu.VMEM((window // 2 - 1, ROUTED, rows, CHUNK_HEADS * DH), values.dtype),
            pltpu.SemaphoreType.DMA((2, window // 2 - 1, ROUTED)),
            pltpu.SemaphoreType.DMA((2, window // 2 - 1, ROUTED)),
            pltpu.SemaphoreType.DMA((2, window // 2 - 1, ROUTED)),
        ],
        compiler_params=pltpu.CompilerParams(
            collective_id=0, has_side_effects=True, vmem_limit_bytes=60 * 1024 * 1024
        ),
    )(doc_blocks, queries, keys, values)


UP, OVER, CROSS, CLIMB, GIFT, RISE, LATE, EXTRA = range(8)


def paired_kernel(
    n,
    docs_hbm,
    q_hbm,
    k_hbm,
    v_hbm,
    o_own,
    q_own,
    own,
    halo,
    transit,
    docs_ref,
    local_sem,
    z_recv,
    y_recv,
    pair_recv,
    cross_recv,
    gift_recv,
    rise_recv,
    send_sem,
):
    me = lax.axis_index("seq")
    place = lax.rem(me, 4)
    row = me // 4
    last_row = n // 4 - 1
    far = place // 2
    core = lax.rem(me, 2)
    partner = me + 1 - 2 * core
    across = me + 2 - 4 * far
    above = me + 4
    below = me - 4
    has_above = above < n
    has_below = below >= 0

    rows, kv_width = k_hbm.shape
    ratio = q_hbm.shape[1] // kv_width
    chunks = kv_width // DH
    last = chunks - 1
    blocks = rows // BLK
    early = jnp.where(core == 0, 3, 1)
    late = 4 - early
    has_far = (far == 1) | has_below
    tops = slice(0, BLK)
    lows = slice(BLK, rows)
    whole = slice(0, rows)

    def routed(of_row):
        return jnp.minimum(chunks, ROUTED_STEP * (last_row - of_row))

    own_first = chunks - routed(row)
    below_first = chunks - routed(row - 1)

    def kv_cols(c, count=1):
        return pl.ds(pl.multiple_of(c * DH, DH), count * DH)

    def remote(src, dst, out, into, device):
        return pltpu.make_async_remote_copy(
            src_ref=src,
            dst_ref=dst,
            send_sem=send_sem.at[out],
            recv_sem=into,
            device_id={"seq": device},
            device_id_type=pl.DeviceIdType.MESH,
        )

    def send_own(slot, c, taken, out, into, device):
        for kind, hbm in enumerate((k_hbm, v_hbm)):
            remote(
                hbm.at[taken, kv_cols(c)],
                halo.at[kind, slot, taken, kv_cols(c)],
                out,
                into,
                device,
            ).start()

    def send_held(src, dst, c, taken, out, into, device):
        remote(
            halo.at[:, src, taken, kv_cols(c)],
            halo.at[:, dst, taken, kv_cols(c)],
            out,
            into,
            device,
        ).start()

    def landed(ref, sem):
        pltpu.make_async_copy(ref, ref, sem).wait()

    def chunk_of(slot, c, taken=whole):
        return halo.at[:, slot, taken, kv_cols(c)]

    def by_half(half, act):
        @pl.when(half)
        def _():
            act(lows)

        @pl.when(jnp.logical_not(half))
        def _():
            act(whole)

    def upward(c):
        half = (place == 0) | ((place == 2) & (c >= own_first))
        by_half(half, lambda taken: send_own(0, c, taken, UP, z_recv.at[c], above))

    def cross_start(c):
        for kind, hbm in enumerate((k_hbm, v_hbm)):
            remote(
                hbm.at[tops, kv_cols(c)],
                transit.at[kind, :, kv_cols(c)],
                CROSS,
                cross_recv.at[c // 2],
                across,
            ).start()

    def climb_start(c):
        remote(
            transit.at[:, :, kv_cols(c)],
            halo.at[:, 2, tops, kv_cols(c)],
            CLIMB,
            y_recv.at[c],
            above,
        ).start()

    barrier = pltpu.get_barrier_semaphore()

    def greet(device):
        pl.semaphore_signal(
            barrier, inc=1, device_id={"seq": device}, device_id_type=pl.DeviceIdType.MESH
        )

    greet(across)

    @pl.when(has_above)
    def _():
        greet(above)

    @pl.when(has_below)
    def _():
        greet(below)

    greet(partner)
    local = [
        pltpu.make_async_copy(k_hbm, own.at[0], local_sem.at[0]),
        pltpu.make_async_copy(v_hbm, own.at[1], local_sem.at[1]),
        pltpu.make_async_copy(q_hbm, q_own, local_sem.at[2]),
    ]
    docs = pltpu.make_async_copy(docs_hbm, docs_ref, local_sem.at[3])
    docs.start()
    for copy in local:
        copy.start()
    pl.semaphore_wait(barrier, 2 + has_above.astype(jnp.int32) + has_below.astype(jnp.int32))

    def first_sends(c, carry):
        @pl.when((place == 1) | ((place == 0) & (c < last)))
        def _():
            send_own(2, c, whole, OVER, y_recv.at[c], across)

        @pl.when(has_above & ((place != 0) | (c < UP_AHEAD)))
        def _():
            upward(c)

        @pl.when((place == 2) & (c < CROSS_AHEAD) & (own_first + c < chunks))
        def _():
            cross_start(own_first + c)

        @pl.when(core == 0)
        def _():
            given = last - c
            send_own(1, given, whole, GIFT, gift_recv.at[(given + 1) // chunks], partner)

        return carry

    lax.fori_loop(0, chunks, first_sends, 0)

    @pl.when(core == 1)
    def _():
        landed(chunk_of(1, last), gift_recv.at[1])

        @pl.when(far == 0)
        def _():
            send_held(1, 3, last, whole, EXTRA, pair_recv.at[last], across)

    @pl.when(jnp.logical_not(has_below))
    def _():
        for r in range(4):

            @pl.when((r == 0) | (r > place))
            def _():
                def clear(i, carry):
                    taken = pl.ds(pl.multiple_of(i * 16, 16), 16)
                    for kind in range(2):
                        halo[kind, r, taken, :] = jnp.zeros((16, kv_width), halo.dtype)
                    return carry

                lax.fori_loop(0, rows // 16, clear, 0)

    def shown(held, first):
        return jnp.concatenate(
            [
                jnp.full((1, BLK), jnp.where(b >= first, 0.0, HIDDEN), jnp.float32)
                for b in held
            ],
            axis=1,
        )

    docs.wait()
    second = jnp.where(place == 2, 1, 2)
    third = jnp.where(place == 2, 2, late)

    def slot_blocks(r):
        return [(me - r) * blocks + b for b in range(blocks)]

    hide_all = []
    hide_main = []
    hide_second = []
    hide_third = []
    for a in range(blocks):
        number = me * blocks + a
        end = jnp.int32(0)
        first = jnp.int32(0)
        for d in range(docs_ref.shape[0]):
            end = end + docs_ref[d]
            first = jnp.where(end <= number, end, first)
        oldest = slot_blocks(4)[a + 1 :]
        mine = slot_blocks(0)[: a + 1]
        between = slot_blocks(3) + slot_blocks(2) + slot_blocks(1)
        hide_all.append(shown(oldest + between + mine, first))
        hide_main.append(shown(oldest + slot_blocks(early) + mine, first))
        hide_second.append(shown(slot_blocks(second), first))
        hide_third.append(shown(slot_blocks(third), first))

    for copy in local:
        copy.wait()

    def heads_of(c):
        return [pl.ds(pl.multiple_of((c * ratio + g) * DH, DH), DH) for g in range(ratio)]

    def query_tile(c, a):
        return jnp.concatenate(
            [q_own[a * BLK : (a + 1) * BLK, hc] for hc in heads_of(c)], axis=0
        )

    def dot_keys(q_tile, keys):
        return lax.dot_general(
            q_tile, keys, (((1,), (1,)), ((), ())), preferred_element_type=jnp.float32
        )

    def gathered(kind, a, slots, cols):
        parts = []
        if a + 1 < blocks:
            parts.append(halo[kind, 0, (a + 1) * BLK :, cols])
        for r in slots:
            parts.append(halo[kind, r, :, cols])
        parts.append(own[kind, : (a + 1) * BLK, cols])
        return jnp.concatenate(parts, axis=0)

    def attend(c, slots, hide):
        q_index = lax.broadcasted_iota(jnp.int32, (BLK, BLK), 0)
        k_index = lax.broadcasted_iota(jnp.int32, (BLK, BLK), 1)
        causal = jnp.where(k_index <= q_index, 0.0, HIDDEN).astype(jnp.float32)
        causal = jnp.concatenate([causal] * ratio, axis=0)
        cols = kv_cols(c)
        kept = []
        for a in range(blocks):
            scores = dot_keys(query_tile(c, a), gathered(0, a, slots, cols)) + hide[a]
            scores = jnp.concatenate([scores[:, :-BLK], scores[:, -BLK:] + causal], axis=1)
            top = jnp.max(scores, axis=1, keepdims=True)
            weights = jnp.exp2((scores - top) * EXP2_SCALE)
            total = jnp.sum(weights, axis=1, keepdims=True)
            blended = jnp.dot(
                weights.astype(jnp.bfloat16),
                gathered(1, a, slots, cols),
                preferred_element_type=jnp.float32,
            )
            kept.append((top, total, blended))
        return kept

    def store(c, kept):
        for a in range(blocks):
            top, total, blended = kept[a]
            blended = (blended / total).astype(o_own.dtype)
            for g, hc in enumerate(heads_of(c)):
                o_own[a * BLK : (a + 1) * BLK, hc] = blended[g * BLK : (g + 1) * BLK]

    def merge(slot, hide, kept):
        merged = []
        cols = kv_cols(last)
        for a in range(blocks):
            top, total, blended = kept[a]
            scores = dot_keys(query_tile(last, a), halo[0, slot, :, cols]) + hide[a]
            new_top = jnp.maximum(top, jnp.max(scores, axis=1, keepdims=True))
            shrink = jnp.exp2((top - new_top) * EXP2_SCALE)
            weights = jnp.exp2((scores - new_top) * EXP2_SCALE)
            total = total * shrink + jnp.sum(weights, axis=1, keepdims=True)
            blended = blended * shrink + jnp.dot(
                weights.astype(jnp.bfloat16),
                halo[1, slot, :, cols],
                preferred_element_type=jnp.float32,
            )
            merged.append((new_top, total, blended))
        return merged

    def z_part(t):
        @pl.when(has_below)
        def _():
            half = (place == 0) | ((place == 2) & (t >= below_first))
            by_half(half, lambda taken: landed(chunk_of(0, t, taken), z_recv.at[t]))

            @pl.when(far == 1)
            def _():
                half = (core == 0) & (t >= below_first)
                by_half(
                    half,
                    lambda taken: send_held(0, 2, t, taken, OVER, y_recv.at[t], across),
                )

            @pl.when((core == 1) & (t < last))
            def _():
                send_held(0, 3, t, whole, RISE, pair_recv.at[t], partner)

            @pl.when((core == 1) & (t == last))
            def _():
                send_held(0, 3, t, whole, RISE, rise_recv.at[0], partner)

        @pl.when(has_above)
        def _():
            ahead = own_first + t + CROSS_AHEAD

            @pl.when((place == 2) & (ahead < chunks))
            def _():
                cross_start(ahead)

            @pl.when((place == 0) & (own_first + t < chunks) & (lax.rem(t, 2) == 0))
            def _():
                c = own_first + t
                landed(transit.at[:, :, kv_cols(c, 2)], cross_recv.at[c // 2])
                climb_start(c)
                climb_start(c + 1)

            @pl.when((place == 0) & (t + UP_AHEAD < chunks))
            def _():
                upward(t + UP_AHEAD)

    def y_part(c):
        @pl.when(has_far)
        def _():
            landed(chunk_of(2, c), y_recv.at[c])
            send_held(2, 4 - late, c, whole, LATE, pair_recv.at[c], partner)

    def attend_all(c):
        both = (core == 0) & has_below

        @pl.when(both)
        def _():
            landed(halo.at[:, 0:2, :, kv_cols(c)], pair_recv.at[c])

        @pl.when(has_far & jnp.logical_not(both))
        def _():
            landed(chunk_of(late, c), pair_recv.at[c])

        store(c, attend(c, (3, 2, 1), hide_all))

    def step_of(t, carry):
        z_part(t)

        @pl.when((t == 2) & (core == 1))
        def _():
            landed(halo.at[:, 1, :, kv_cols(0, last)], gift_recv.at[0])

        @pl.when(t >= 2)
        def _():
            attend_all(t - 2)

        @pl.when(t >= 1)
        def _():
            y_part(t - 1)

        return carry

    lax.fori_loop(0, last, step_of, 0)
    z_part(last)
    attend_all(last - 2)

    @pl.when((core == 0) & has_below)
    def _():
        landed(chunk_of(3, last), rise_recv.at[0])

    kept = attend(last, (early,), hide_main)
    y_part(last - 1)
    attend_all(last - 1)

    @pl.when(has_far & (place != 2))
    def _():
        landed(chunk_of(2, last), y_recv.at[last])
        send_held(2, 4 - late, last, whole, LATE, pair_recv.at[last], partner)

    @pl.when(place == 2)
    def _():
        landed(chunk_of(1, last), pair_recv.at[last])

    kept = merge(second, hide_second, kept)

    @pl.when(has_far & (place != 2))
    def _():
        landed(chunk_of(late, last), pair_recv.at[last])

        @pl.when(place == 3)
        def _():
            send_held(3, 2, last, whole, EXTRA, y_recv.at[last], partner)

    @pl.when(place == 2)
    def _():
        landed(chunk_of(2, last), y_recv.at[last])

    store(last, merge(third, hide_third, kept))

    def drained(taken, width, out):
        landed(halo.at[:, 0, taken, 0:width], send_sem.at[out])

    @pl.when(has_above & (place == 0))
    def _():
        drained(lows, kv_width, UP)

    @pl.when(has_above & (core == 1))
    def _():
        drained(whole, kv_width, UP)

    @pl.when((place == 1) | ((place == 3) & has_below))
    def _():
        drained(whole, kv_width, OVER)

    @pl.when(place == 0)
    def _():
        drained(whole, last * DH, OVER)

    for r in range(last_row):
        count = min(chunks, ROUTED_STEP * (last_row - r))

        @pl.when((place == 2) & (row == r))
        def _():
            drained(whole, (2 * chunks - count) * DH // 2, UP)
            drained(tops, count * DH, CROSS)

        @pl.when((place == 2) & (row == r + 1))
        def _():
            drained(whole, (2 * chunks - count) * DH // 2, OVER)

        @pl.when((place == 0) & (row == r))
        def _():
            drained(tops, count * DH, CLIMB)

    @pl.when(core == 0)
    def _():
        drained(whole, kv_width, GIFT)

    @pl.when((core == 1) & has_below)
    def _():
        drained(whole, kv_width, RISE)

    @pl.when(has_far & (place != 2))
    def _():
        drained(whole, kv_width, LATE)

    @pl.when(place == 2)
    def _():
        drained(whole, last * DH, LATE)

    @pl.when(core == 1)
    def _():
        drained(whole, DH, EXTRA)


def on_paired_device(n, queries, keys, values, doc_blocks):
    rows, kv_width = keys.shape
    chunks = kv_width // DH
    return pl.pallas_call(
        functools.partial(paired_kernel, n),
        out_shape=pltpu.VMEM(queries.shape, queries.dtype),
        in_specs=[pl.BlockSpec(memory_space=pl.ANY)] * 4,
        out_specs=pl.BlockSpec(memory_space=pltpu.VMEM),
        scratch_shapes=[
            pltpu.VMEM(queries.shape, queries.dtype),
            pltpu.VMEM((2, rows, kv_width), keys.dtype),
            pltpu.VMEM((2, 4, rows, kv_width), keys.dtype),
            pltpu.VMEM((2, BLK, kv_width), keys.dtype),
            pltpu.SMEM(doc_blocks.shape, doc_blocks.dtype),
            pltpu.SemaphoreType.DMA((4,)),
            pltpu.SemaphoreType.DMA((chunks,)),
            pltpu.SemaphoreType.DMA((chunks,)),
            pltpu.SemaphoreType.DMA((chunks,)),
            pltpu.SemaphoreType.DMA((chunks // 2,)),
            pltpu.SemaphoreType.DMA((2,)),
            pltpu.SemaphoreType.DMA((1,)),
            pltpu.SemaphoreType.DMA((8,)),
        ],
        compiler_params=pltpu.CompilerParams(
            collective_id=0, has_side_effects=True, vmem_limit_bytes=60 * 1024 * 1024
        ),
    )(doc_blocks, queries, keys, values)


def solution(mesh):
    n = mesh.shape["seq"]
    spread = P(("groups", "seq"), None)
    return jax.shard_map(
        functools.partial(on_paired_device if n // 4 == 4 else on_device, n),
        mesh=mesh,
        in_specs=(spread, spread, spread, P("groups")),
        out_specs=spread,
        check_vma=False,
    )
```

profile of v0, /device:TPU:25, one launch (start us, length us, event | category | flops | bytes accessed | tf_op | source)
XLA Modules:
  0.0 55.7 jit_solution(15723479865110289276)
XLA Ops:
  0.0 54.4 %shard_map.46 = bf16[256,4096]{1,0:T(8,128)(2,1)S(1)} custom-call(s32[8]{0:T(128)} %docs_hbm.1, bf16[256,4096]{1,0:T(8,128)(2,1)} %q_hbm.1, bf16[256,2048]{1,0:T(8,128)(2,1)} %k_hbm.1, bf16[256,2048]{1,0:T(8,128)(2,1)} %v_hbm.1), custom_call_target="tpu_custom_call" | custom-call | tf_op jit(solution)/shard_map/pallas_call | solution.py:883
  54.4 1.3 %copy.6 = bf16[256,4096]{1,0:T(8,128)(2,1)} copy(bf16[256,4096]{1,0:T(8,128)(2,1)S(1)} %shard_map.46) | data formatting | bytes 4194304
where the time goes:
time: 55.9 us; the launch traced here: 55.7 us
  Pallas kernels  54.4 us (97%)
  local copies, waits for them, and re-layouts  1.32 us (2%)
    pallas_call x1, Pallas kernels, on_paired_device(): pl.pallas_call(functools.partial(paired_kernel, n), out_shape=pltpu.VMEM(...  54.4 us
    unnamed x1, local copies, waits for them, and re-layouts  1.32 us

commit v1 on v0

--- a/solution.py
+++ b/solution.py
@@ -13,9 +13,12 @@
 ROUTED = 1
 EXP2_SCALE = 144.0 ** (-0.5) * 1.4426950408889634
 HIDDEN = -1e30
-ROUTED_STEP = 6
+ROUTED_STEP = 4
+ROUTED_BASE = 0
+ROUTED_SPARE = 2
 CROSS_AHEAD = 4
 UP_AHEAD = 3
+Z_LEAD = 1
 
 
 def kernel(
@@ -453,7 +456,10 @@
     whole = slice(0, rows)
 
     def routed(of_row):
-        return jnp.minimum(chunks, ROUTED_STEP * (last_row - of_row))
+        higher = last_row - of_row
+        return jnp.where(
+            higher > 0, jnp.minimum(chunks - ROUTED_SPARE, ROUTED_STEP * higher + ROUTED_BASE), 0
+        )
 
     own_first = chunks - routed(row)
     below_first = chunks - routed(row - 1)
@@ -477,7 +483,7 @@
                 hbm.at[taken, kv_cols(c)],
                 halo.at[kind, slot, taken, kv_cols(c)],
                 out,
-                into,
+                into(kind),
                 device,
             ).start()
 
@@ -507,7 +513,7 @@
 
     def upward(c):
         half = (place == 0) | ((place == 2) & (c >= own_first))
-        by_half(half, lambda taken: send_own(0, c, taken, UP, z_recv.at[c], above))
+        by_half(half, lambda taken: send_own(0, c, taken, UP, lambda kind: z_recv.at[kind, c], above))
 
     def cross_start(c):
         for kind, hbm in enumerate((k_hbm, v_hbm)):
@@ -560,9 +566,9 @@
     def first_sends(c, carry):
         @pl.when((place == 1) | ((place == 0) & (c < last)))
         def _():
-            send_own(2, c, whole, OVER, y_recv.at[c], across)
-
-        @pl.when(has_above & ((place != 0) | (c < UP_AHEAD)))
+            send_own(2, c, whole, OVER, lambda kind: y_recv.at[c], across)
+
+        @pl.when(has_above & ((core == 1) | (c < UP_AHEAD)))
         def _():
             upward(c)
 
@@ -573,7 +579,8 @@
         @pl.when(core == 0)
         def _():
             given = last - c
-            send_own(1, given, whole, GIFT, gift_recv.at[(given + 1) // chunks], partner)
+            into = gift_recv.at[(given + 1) // chunks]
+            send_own(1, given, whole, GIFT, lambda kind: into, partner)
 
         return carry
 
@@ -711,15 +718,23 @@
         @pl.when(has_below)
         def _():
             half = (place == 0) | ((place == 2) & (t >= below_first))
-            by_half(half, lambda taken: landed(chunk_of(0, t, taken), z_recv.at[t]))
-
-            @pl.when(far == 1)
-            def _():
-                half = (core == 0) & (t >= below_first)
-                by_half(
-                    half,
-                    lambda taken: send_held(0, 2, t, taken, OVER, y_recv.at[t], across),
-                )
+            for kind in range(2):
+
+                def pass_on(taken):
+                    held = halo.at[kind, 0, taken, kv_cols(t)]
+                    landed(held, z_recv.at[kind, t])
+
+                    @pl.when(far == 1)
+                    def _():
+                        remote(
+                            held,
+                            halo.at[kind, 2, taken, kv_cols(t)],
+                            OVER,
+                            y_recv.at[t],
+                            across,
+                        ).start()
+
+                by_half(half, pass_on)
 
             @pl.when((core == 1) & (t < last))
             def _():
@@ -744,7 +759,7 @@
                 climb_start(c)
                 climb_start(c + 1)
 
-            @pl.when((place == 0) & (t + UP_AHEAD < chunks))
+            @pl.when((core == 0) & (t + UP_AHEAD < chunks))
             def _():
                 upward(t + UP_AHEAD)
 
@@ -767,8 +782,20 @@
 
         store(c, attend(c, (3, 2, 1), hide_all))
 
+    def z_lead(t, carry):
+        z_part(t)
+        return carry
+
+    lax.fori_loop(0, Z_LEAD, z_lead, 0)
+
     def step_of(t, carry):
-        z_part(t)
+        @pl.when(t + Z_LEAD < chunks)
+        def _():
+            z_part(t + Z_LEAD)
+
+        @pl.when(t >= 1)
+        def _():
+            y_part(t - 1)
 
         @pl.when((t == 2) & (core == 1))
         def _():
@@ -778,14 +805,14 @@
         def _():
             attend_all(t - 2)
 
-        @pl.when(t >= 1)
-        def _():
-            y_part(t - 1)
-
         return carry
 
     lax.fori_loop(0, last, step_of, 0)
-    z_part(last)
+
+    @pl.when(Z_LEAD == 0)
+    def _():
+        z_part(last)
+
     attend_all(last - 2)
 
     @pl.when((core == 0) & has_below)
@@ -841,7 +868,7 @@
         drained(whole, last * DH, OVER)
 
     for r in range(last_row):
-        count = min(chunks, ROUTED_STEP * (last_row - r))
+        count = min(chunks - ROUTED_SPARE, ROUTED_STEP * (last_row - r) + ROUTED_BASE)
 
         @pl.when((place == 2) & (row == r))
         def _():
@@ -892,7 +919,7 @@
             pltpu.VMEM((2, BLK, kv_width), keys.dtype),
             pltpu.SMEM(doc_blocks.shape, doc_blocks.dtype),
             pltpu.SemaphoreType.DMA((4,)),
-            pltpu.SemaphoreType.DMA((chunks,)),
+            pltpu.SemaphoreType.DMA((2, chunks)),
             pltpu.SemaphoreType.DMA((chunks,)),
             pltpu.SemaphoreType.DMA((chunks,)),
             pltpu.SemaphoreType.DMA((chunks // 2,)),

time: 55.9 us -> 54.4 us (0.973)
  Pallas kernels: 54.4 us -> 52.9 us
    pallas_call x1, Pallas kernels: 54.4 us -> 52.9 us  [on_paired_device(): pl.pallas_call(functools.partial(paired_kernel, n), out_shape=pltpu.VMEM(...]
where the time goes in v1:
time: 54.4 us; the launch traced here: 54.3 us
  Pallas kernels  52.9 us (97%)
  local copies, waits for them, and re-layouts  1.32 us (2%)
    pallas_call x1, Pallas kernels, on_paired_device(): pl.pallas_call(functools.partial(paired_kernel, n), out_shape=pltpu.VMEM(...  52.9 us
    unnamed x1, local copies, waits for them, and re-layouts  1.32 us

profile of v1, /device:TPU:25, one launch (start us, length us, event | category | flops | bytes accessed | tf_op | source)
XLA Modules:
  0.0 54.3 jit_solution(16716228612685911679)
XLA Ops:
  0.0 52.9 %shard_map.46 = bf16[256,4096]{1,0:T(8,128)(2,1)S(1)} custom-call(s32[8]{0:T(128)} %docs_hbm.1, bf16[256,4096]{1,0:T(8,128)(2,1)} %q_hbm.1, bf16[256,2048]{1,0:T(8,128)(2,1)} %k_hbm.1, bf16[256,2048]{1,0:T(8,128)(2,1)} %v_hbm.1), custom_call_target="tpu_custom_call" | custom-call | tf_op jit(solution)/shard_map/pallas_call | solution.py:910
  52.9 1.3 %copy.6 = bf16[256,4096]{1,0:T(8,128)(2,1)} copy(bf16[256,4096]{1,0:T(8,128)(2,1)S(1)} %shard_map.46) | data formatting | bytes 4194304
